TPU v7x, 32 devices: a whole 2x2x4 slice. The times are simulated.
32 devices in a mesh: row: 4 (over x, core), col: 8 (over z, y).
Axes of the slice: x: 2, y: 2, z: 4, core: 2. Of those that a mesh axis runs over, the one named last changes fastest.
Arguments:
- matrix: float32 [2048, 2048], P('row', 'col'), as said below
- start_vectors: float32 [2048, 512], P(('col', 'row')), may hold values from -6 to 6
- interval: float32 [2], replicated, as said below
Outputs:
- ortho_basis: float32 [2048, 512], P(('col', 'row'))
- projected: float32 [512, 512], replicated
- residual: float32 [2048, 512], P(('col', 'row'))
Inputs may be any that keep to these rules, and one draw needn't show every extreme that they name: matrix is exactly symmetric (entry (r, c) equals entry (c, r)); its eigenvalues lie within about -1.45 to 1.45. interval[0] lies in [-1.2, -0.7] and interval[1] in [1.45, 1.9].
All inputs are finite; a program needn't handle non-finite values.
Results may differ from a plain program's by a relative error of at most 0.0003.
Values sent between devices are 32-bit elements.
A program may use at most 128 MiB of HBM per device.

v0:
```python
import jax
import jax.numpy as jnp
from jax import lax
from jax.sharding import PartitionSpec as P

FILTER_DEG = 3
OUTER = 2


def scattered(contribution, width, axis):
    whole = contribution(jnp.int32(0), width * lax.axis_size(axis))
    return lax.psum_scatter(whole, axis, scatter_dimension=0, tiled=True)


def spread(array, axis, root):
    mine = lax.axis_index(axis) == root
    return lax.psum(jnp.where(mine, array, jnp.zeros_like(array)), axis)


def product(left, right):
    return jnp.dot(left, right, precision=lax.Precision.HIGHEST, preferred_element_type=jnp.float32)


def tri_solve(factor, values):
    return jax.scipy.linalg.solve_triangular(factor, values, lower=True)


def on_device(matrix, start_vectors, interval):
    block_rows, block_cols = matrix.shape
    slab_rows = start_vectors.shape[0]
    total_rows = slab_rows * lax.axis_size("row") * lax.axis_size("col")
    row_index = lax.axis_index("row")
    col_index = lax.axis_index("col")
    center = 0.5 * (interval[0] + interval[1])
    half_width = 0.5 * (interval[1] - interval[0])
    global_rows = row_index * block_rows + lax.iota(jnp.int32, block_rows)
    global_cols = col_index * block_cols + lax.iota(jnp.int32, block_cols)
    diagonal = global_rows[:, None] == global_cols[None, :]
    shifted = jnp.where(diagonal, matrix - center, matrix) / half_width

    def forward(col_full):

        def term(first_row, row_count):
            strip = lax.dynamic_slice_in_dim(shifted, first_row, row_count, 0)
            return product(strip, col_full)

        return scattered(term, slab_rows, "col")

    def gather_rows(slab_part):
        return lax.all_gather(slab_part, "col", axis=0, tiled=True)

    def to_columns(row_full):
        root_row = col_index * block_cols // block_rows
        offset = col_index * block_cols - root_row * block_rows
        column_part = lax.dynamic_slice_in_dim(row_full, offset, block_cols, 0)
        return spread(column_part, "row", root_row)

    def backward(row_full):
        partial_value = lax.dot_general(
            shifted,
            row_full,
            (((0,), (0,)), ((), ())),
            precision=lax.Precision.HIGHEST,
            preferred_element_type=jnp.float32,
        )
        return lax.psum(partial_value, "row")

    current_start = lax.all_gather(start_vectors, "row", axis=0, tiled=True)
    for sweep_index in range(OUTER):
        even_cols = current_start
        odd_slab = forward(current_start)
        odd_rows = gather_rows(odd_slab)
        for degree in range(2, FILTER_DEG + 1):
            if degree % 2 == 0:
                even_cols = 2.0 * backward(odd_rows) - even_cols
            else:
                odd_slab = 2.0 * forward(even_cols) - odd_slab
                odd_rows = gather_rows(odd_slab)
        final_cols = to_columns(odd_rows)
        mapped_cols = backward(odd_rows)
        final_slab = lax.dynamic_slice_in_dim(final_cols, row_index * slab_rows, slab_rows, 0)
        mapped_slab = lax.dynamic_slice_in_dim(mapped_cols, row_index * slab_rows, slab_rows, 0)
        gram_part = product(final_slab.T, final_slab)
        cross_part = product(final_slab.T, mapped_slab)
        gram_total = lax.psum(gram_part, ("row", "col"))
        cross_total = lax.psum(cross_part, ("row", "col"))
        gram_matrix = gram_total / total_rows
        cross_terms = cross_total / total_rows
        factor = jnp.linalg.cholesky(gram_matrix)
        basis_cols = tri_solve(factor, final_cols.T).T
        partial_proj = tri_solve(factor, cross_terms)
        projected = tri_solve(factor, partial_proj.T).T
        current_start = basis_cols
    basis_slab = lax.dynamic_slice_in_dim(current_start, row_index * slab_rows, slab_rows, 0)
    residual = tri_solve(factor, mapped_slab.T).T - product(basis_slab, projected)
    return (basis_slab, projected, residual)


def solution(mesh):
    return jax.shard_map(
        on_device,
        mesh=mesh,
        in_specs=(P("row", "col"), P(("col", "row"), None), P()),
        out_specs=(P(("col", "row"), None), P(), P(("col", "row"), None)),
        check_vma=False,
    )
```

profile of v0, /device:TPU:0, one launch (start us, length us, event | category | flops | bytes accessed | tf_op | source)
XLA Modules:
  0.0 1179.7 jit_solution(1612085924572650123)
XLA Ops:
  11.0 8.9 all_gather.15
  19.9 2.1 fusion.159
  22.0 65.1 %reduce-scatter.5.cloned.1.call-done = f32[64,512]{1,0:T(8,128)} async-done(((f32[512,512]{1,0:T(8,128)}), f32[64,512]{1,0:T(8,128)}) %reduce-scatter.5.cloned.1.call-update) | async-done | bytes 131088 | tf_op jit(solution)/shard_map/reduce_scatter | solution.py:12
  87.2 41.3 %all-gather.5.cloned.1.call-done = f32[512,512]{1,0:T(8,128)} async-done(((f32[64,512]{1,0:T(8,128)}), f32[512,512]{1,0:T(8,128)}) %all-gather.5.cloned.1.call-update) | async-done | bytes 1048592 | tf_op jit(solution)/shard_map/all_gather | solution.py:50
  128.5 3.9 fusion.157
  132.7 32.0 %all-reduce.10.cloned.1.call-done = f32[256,512]{0,1:T(8,128)} async-done(((f32[256,512]{0,1:T(8,128)}), f32[256,512]{0,1:T(8,128)}) %all-reduce.10.cloned.1.call-update) | async-done | bytes 524304 | tf_op jit(solution)/shard_map/psum | solution.py:66
  164.7 3.1 fusion.22
  167.9 65.6 %reduce-scatter.7.cloned.1.call-done = f32[64,512]{1,0:T(8,128)} async-done(((f32[512,512]{1,0:T(8,128)}), f32[64,512]{1,0:T(8,128)}) %reduce-scatter.7.cloned.1.call-update) | async-done | bytes 131088 | tf_op jit(solution)/shard_map/reduce_scatter | solution.py:12
  233.6 1.6 multiply_subtract_fusion.1
  235.3 40.1 %all-gather.7.cloned.1.call-done = f32[512,512]{1,0:T(8,128)} async-done(((f32[64,512]{1,0:T(8,128)}), f32[512,512]{1,0:T(8,128)}) %all-gather.7.cloned.1.call-update) | async-done | bytes 1048592 | tf_op jit(solution)/shard_map/all_gather | solution.py:50
  275.4 1.9 dynamic-slice_select_fusion.1
  277.3 33.0 %all-reduce.12.cloned.1.call-done = f32[256,512]{1,0:T(8,128)} async-done(((f32[256,512]{1,0:T(8,128)}), f32[256,512]{1,0:T(8,128)}) %all-reduce.12.cloned.1.call-update) | async-done | bytes 524304 | tf_op jit(solution)/shard_map/psum | solution.py:17
  310.3 3.0 fusion.73
  313.5 133.4 %all-reduce.14.cloned.1.call-done = f32[512,512]{0,1:T(8,128)} async-done(((f32[512,512]{0,1:T(8,128)}), f32[512,512]{0,1:T(8,128)}) %all-reduce.14.cloned.1.call-update) | async-done | bytes 1048592 | tf_op jit(solution)/shard_map/psum | solution.py:85
  446.9 1.3 broadcast_multiply_fusion.2
  448.6 0.9 copy-done.1
  449.7 11.7 cholesky.286
  461.5 9.8 custom-call.36
  472.1 11.7 cholesky.305
  483.8 10.0 custom-call.37
  494.5 11.7 cholesky.326
  507.0 9.8 custom-call.38
  517.4 11.7 cholesky.343
  529.8 1.1 compare_reduce_fusion.6
  533.6 8.5 while.9
  534.2 1.4 bitcast_dynamic-update-slice_fusion.4
  536.4 1.4 bitcast_dynamic-update-slice_fusion.4
  538.5 1.4 bitcast_dynamic-update-slice_fusion.4
  540.6 1.4 bitcast_dynamic-update-slice_fusion.4
  542.1 39.3 %custom-call.39 = f32[4,128,128]{1,2,0:T(8,128)S(1)} custom-call(f32[4,128,128]{2,1,0:T(8,128)S(1)} %get-tuple-element.42), custom_call_target="InvertDiagBlocksLowerTriangular" | custom-call | tf_op jit(solution)/shard_map/jit(_solve_triangular)/triangular_solve | solution.py:25
  584.5 2.1 fusion.35
  586.6 63.4 %reduce-scatter.9.cloned.1.call-done = f32[64,512]{1,0:T(8,128)} async-done(((f32[512,512]{1,0:T(8,128)}), f32[64,512]{1,0:T(8,128)}) %reduce-scatter.9.cloned.1.call-update) | async-done | bytes 131088 | tf_op jit(solution)/shard_map/reduce_scatter | solution.py:12
  650.1 41.3 %all-gather.9.cloned.1.call-done = f32[512,512]{1,0:T(8,128)} async-done(((f32[64,512]{1,0:T(8,128)}), f32[512,512]{1,0:T(8,128)}) %all-gather.9.cloned.1.call-update) | async-done | bytes 1048592 | tf_op jit(solution)/shard_map/all_gather | solution.py:50
  691.4 3.9 fusion.153
  695.4 32.2 %all-reduce.16.cloned.1.call-done = f32[256,512]{0,1:T(8,128)} async-done(((f32[256,512]{0,1:T(8,128)}), f32[256,512]{0,1:T(8,128)}) %all-reduce.16.cloned.1.call-update) | async-done | bytes 524304 | tf_op jit(solution)/shard_map/psum | solution.py:66
  727.6 3.1 fusion.20
  730.8 65.8 %reduce-scatter.11.cloned.1.call-done = f32[64,512]{1,0:T(8,128)} async-done(((f32[512,512]{1,0:T(8,128)}), f32[64,512]{1,0:T(8,128)}) %reduce-scatter.11.cloned.1.call-update) | async-done | bytes 131088 | tf_op jit(solution)/shard_map/reduce_scatter | solution.py:12
  796.5 1.6 multiply_subtract_fusion
  798.2 40.2 %all-gather.11.cloned.1.call-done = f32[512,512]{1,0:T(8,128)} async-done(((f32[64,512]{1,0:T(8,128)}), f32[512,512]{1,0:T(8,128)}) %all-gather.11.cloned.1.call-update) | async-done | bytes 1048592 | tf_op jit(solution)/shard_map/all_gather | solution.py:50
  838.4 3.3 fusion.150
  842.8 35.0 %all-reduce.20.cloned.1.call-done = (f32[256,512]{1,0:T(8,128)}, f32[256,512]{1,0:T(8,128)}) async-done(((f32[256,512]{1,0:T(8,128)}, f32[256,512]{1,0:T(8,128)}), (f32[256,512]{1,0:T(8,128)}, f32[256,512]{1,0:T(8,128)})) %all-reduce.20.cloned.1.call-update) | async-done | bytes 1048592 | tf_op jit(solution)/shard_map/psum | solution.py:17
  877.8 3.0 fusion.78
  880.8 2.9 fusion.75
  883.7 135.3 %all-reduce.18.cloned.1.call-done = (f32[512,512]{0,1:T(8,128)}, f32[512,512]{0,1:T(8,128)}) async-done(((f32[512,512]{0,1:T(8,128)}, f32[512,512]{0,1:T(8,128)}), (f32[512,512]{0,1:T(8,128)}, f32[512,512]{0,1:T(8,128)})) %all-reduce.18.cloned.1.call-update) | async-done | bytes 2097168 | tf_op jit(solution)/shard_map/psum | solution.py:85
  1019.0 2.4 broadcast_multiply_fusion
  1022.1 11.7 cholesky.358
  1034.5 9.8 custom-call.40
  1045.1 12.1 %cholesky.377 = f32[128,128]{1,0:T(8,128)S(1)} custom-call(f32[128,128]{1,0:T(8,128)S(1)} %cholesky.443), custom_call_target="Cholesky" | custom-call | tf_op jit(solution)/shard_map/jit(cholesky)/cholesky | solution.py:89
  1057.9 9.8 custom-call.41
  1068.4 11.7 cholesky.398
  1080.8 9.8 custom-call.42
  1091.2 11.7 cholesky.415
  1106.3 8.5 while.10
  1107.0 1.4 bitcast_dynamic-update-slice_fusion.5
  1109.1 1.4 bitcast_dynamic-update-slice_fusion.5
  1111.2 1.4 bitcast_dynamic-update-slice_fusion.5
  1113.4 1.4 bitcast_dynamic-update-slice_fusion.5
  1114.8 39.5 %custom-call.43 = f32[4,128,128]{1,2,0:T(8,128)S(1)} custom-call(f32[4,128,128]{2,1,0:T(8,128)S(1)} %get-tuple-element.43), custom_call_target="InvertDiagBlocksLowerTriangular" | custom-call | tf_op jit(solution)/shard_map/jit(_solve_triangular)/triangular_solve | solution.py:25
  1161.5 1.0 convolution_subtract_fusion.2
  1163.0 1.5 convolution_subtract_fusion.5
  1166.4 1.0 convolution_subtract_fusion
  1167.8 1.5 convolution_subtract_fusion.4
  1169.9 1.8 convolution_subtract_fusion.16
  1171.7 1.3 copy.21
  (153 shorter events, 32.0 us)
Async XLA Ops:
  7.2 0.7 copy-start.9
  7.2 12.7 %copy-start.10 = (f32[512,256]{1,0:T(8,128)S(1)}, f32[512,256]{1,0:T(8,128)}, u32[]{:S(2)}) copy-start(f32[512,256]{1,0:T(8,128)} %param.8) | copy-start | bytes 1572868
  7.2 80.0 %reduce-scatter.5.cloned.1.call-start = ((), (), s32[]{:S(2)}) async-start(), calls=%async_computation.4 | async-start | bytes 1179648 | tf_op jit(solution)/shard_map/reduce_scatter | solution.py:12
  22.0 106.6 %all-gather.5.cloned.1.call-start = ((), (), s32[]{:S(2)}) async-start(), calls=%async_computation.5 | async-start | bytes 1179648 | tf_op jit(solution)/shard_map/all_gather | solution.py:50
  87.2 77.6 %all-reduce.10.cloned.1.call-start = ((), (), s32[]{:S(2)}) async-start(), calls=%async_computation.6 | async-start | bytes 1048576 | tf_op jit(solution)/shard_map/psum | solution.py:66
  132.5 101.1 %reduce-scatter.7.cloned.1.call-start = ((), (), s32[]{:S(2)}) async-start(), calls=%async_computation.7 | async-start | bytes 1179648 | tf_op jit(solution)/shard_map/reduce_scatter | solution.py:12
  167.9 65.7 %copy-start.6 = (f32[64,512]{1,0:T(8,128)S(1)}, f32[64,512]{1,0:T(8,128)}, u32[]{:S(2)}) copy-start(f32[64,512]{1,0:T(8,128)} %reduce-scatter.5.cloned.1.call-done) | copy-start | bytes 393220
  167.9 107.5 %all-gather.7.cloned.1.call-start = ((), (), s32[]{:S(2)}) async-start(), calls=%async_computation.8 | async-start | bytes 1179648 | tf_op jit(solution)/shard_map/all_gather | solution.py:50
  235.2 75.1 %all-reduce.12.cloned.1.call-start = ((), (), s32[]{:S(2)}) async-start(), calls=%async_computation.9 | async-start | bytes 1048576 | tf_op jit(solution)/shard_map/psum | solution.py:17
  277.3 169.7 %all-reduce.14.cloned.1.call-start = ((), (), s32[]{:S(2)}) async-start(), calls=%async_computation.10 | async-start | bytes 2097152 | tf_op jit(solution)/shard_map/psum | solution.py:85
  313.3 336.7 %reduce-scatter.9.cloned.1.call-start = ((), (), s32[]{:S(2)}) async-start(), calls=%async_computation.11 | async-start | bytes 1179648 | tf_op jit(solution)/shard_map/reduce_scatter | solution.py:12
  448.3 1.2 copy-start.1
  533.4 48.0 %copy-start.4 = (f32[256,512]{1,0:T(8,128)S(1)}, f32[256,512]{1,0:T(8,128)}, u32[]{:S(2)}) copy-start(f32[256,512]{1,0:T(8,128)} %all-reduce.12.cloned.1.call-done) | copy-start | bytes 1572868
  583.3 1.2 copy-start.11
  586.6 104.8 %all-gather.9.cloned.1.call-start = ((), (), s32[]{:S(2)}) async-start(), calls=%async_computation.12 | async-start | bytes 1179648 | tf_op jit(solution)/shard_map/all_gather | solution.py:50
  650.0 77.6 %all-reduce.16.cloned.1.call-start = ((), (), s32[]{:S(2)}) async-start(), calls=%async_computation.13 | async-start | bytes 1048576 | tf_op jit(solution)/shard_map/psum | solution.py:66
  695.3 101.2 %reduce-scatter.11.cloned.1.call-start = ((), (), s32[]{:S(2)}) async-start(), calls=%async_computation.14 | async-start | bytes 1179648 | tf_op jit(solution)/shard_map/reduce_scatter | solution.py:12
  730.7 65.8 %copy-start.5 = (f32[64,512]{1,0:T(8,128)S(1)}, f32[64,512]{1,0:T(8,128)}, u32[]{:S(2)}) copy-start(f32[64,512]{1,0:T(8,128)} %reduce-scatter.9.cloned.1.call-done) | copy-start | bytes 393220
  730.7 107.6 %all-gather.11.cloned.1.call-start = ((), (), s32[]{:S(2)}) async-start(), calls=%async_computation.15 | async-start | bytes 1179648 | tf_op jit(solution)/shard_map/all_gather | solution.py:50
  798.2 79.6 %all-reduce.20.cloned.1.call-start = ((), (), s32[]{:S(2)}) async-start(), calls=%async_computation.17 | async-start | bytes 2097152 | tf_op jit(solution)/shard_map/psum | solution.py:17
  838.4 3.3 copy-start.7
  842.6 176.4 %all-reduce.18.cloned.1.call-start = ((), (), s32[]{:S(2)}) async-start(), calls=%async_computation.16 | async-start | bytes 4194304 | tf_op jit(solution)/shard_map/psum | solution.py:85
  877.8 3.0 copy-start.8
  1019.0 2.4 copy-start
  1154.7 1.3 copy-start.3
  1158.0 2.1 copy-start.2
Sparse Core Ops, SparseCore 0:
  22.1 65.0 reduce-scatter.4
  89.3 39.2 all-gather.4
  132.6 32.0 all-reduce.9
  168.6 64.9 reduce-scatter.6
  236.1 39.1 all-gather.6
  278.2 32.0 all-reduce.11
  316.1 130.8 all-reduce.13
  586.7 63.2 reduce-scatter.8
  652.1 39.2 all-gather.8
  695.4 32.1 all-reduce.15
  731.6 64.9 reduce-scatter.10
  799.1 39.2 all-gather.10
  842.7 35.0 all-reduce.19
  883.8 135.1 all-reduce.17
where the time goes:
time: 1190 us; the launch traced here: 1180 us
  waiting for transfers between devices  824 us (69%)
  other arithmetic  248 us (21%)
  matrix products  53.3 us (4%)
  between operations  22.6 us (2%)
  local copies, waits for them, and re-layouts  22.2 us (2%)
    psum x2, waiting for transfers between devices, on_device(): gram_total = lax.psum(gram_part, ('row', 'col'))  269 us
    reduce_scatter x4, waiting for transfers between devices, scattered(): return lax.psum_scatter(whole, axis, scatter_dimension=0, tiled=True)  260 us
    all_gather x4, waiting for transfers between devices, gather_rows(): return lax.all_gather(slab_part, 'col', axis=0, tiled=True)  163 us
    another operation x29, other arithmetic, on_device(): factor = jnp.linalg.cholesky(gram_matrix)  158 us
    another operation x6, other arithmetic, tri_solve(): return jax.scipy.linalg.solve_triangular(factor, values, lower=True)  79.2 us
    psum x2, waiting for transfers between devices, spread(): return lax.psum(jnp.where(mine, array, jnp.zeros_like(array)), axis)  67.9 us
    psum x2, waiting for transfers between devices, backward(): return lax.psum(partial_value, 'row')  64.2 us
  transfers between devices with their start and end apart: 14, of which 14 were waited for; matrix products, arithmetic and copies ran while one was open for 0% of the time, Pallas kernels for 0%

commit v1 on v0

--- a/solution.py
+++ b/solution.py
@@ -82,7 +82,8 @@
         mapped_slab = lax.dynamic_slice_in_dim(mapped_cols, row_index * slab_rows, slab_rows, 0)
         gram_part = product(final_slab.T, final_slab)
         cross_part = product(final_slab.T, mapped_slab)
-        gram_total = lax.psum(gram_part, ("row", "col"))
+        parts = lax.all_gather(gram_part, ("row", "col"), axis=0, tiled=False)
+        gram_total = parts.sum(axis=0)
         cross_total = lax.psum(cross_part, ("row", "col"))
         gram_matrix = gram_total / total_rows
         cross_terms = cross_total / total_rows

time: 1190 us -> 1470 us (1.24)
  waiting for transfers between devices: 824 us -> 1070 us
  other arithmetic: 248 us -> 273 us
    all_gather x0 -> x2, waiting for transfers between devices: none -> 389 us  [on_device(): parts = lax.all_gather(gram_part, ('row', 'col'), axis=0, tiled=False)]
    psum x2 -> x1, waiting for transfers between devices: 269 us -> 129 us  [on_device(): cross_total = lax.psum(cross_part, ('row', 'col'))]
    reduce_sum x0 -> x2, other arithmetic: none -> 25.1 us  [on_device(): gram_total = parts.sum(axis=0)]
  transfers between devices with their start and end apart: 14 -> 15, of which waited for: 14 -> 15; matrix products, arithmetic and copies ran while one was open for 0% -> 0% of each run, Pallas kernels for 0% -> 0%
where the time goes in v1:
time: 1470 us
  waiting for transfers between devices  1070 us (73%)
  other arithmetic  273 us (19%)
  matrix products  67 us (5%)
  local copies, waits for them, and re-layouts  22.5 us (2%)
  between operations  22.5 us (2%)
    all_gather x2, waiting for transfers between devices, on_device(): parts = lax.all_gather(gram_part, ('row', 'col'), axis=0, tiled=False)  389 us
    reduce_scatter x4, waiting for transfers between devices, scattered(): return lax.psum_scatter(whole, axis, scatter_dimension=0, tiled=True)  259 us
    all_gather x4, waiting for transfers between devices, gather_rows(): return lax.all_gather(slab_part, 'col', axis=0, tiled=True)  163 us
    another operation x29, other arithmetic, on_device(): factor = jnp.linalg.cholesky(gram_matrix)  158 us
    psum x1, waiting for transfers between devices, on_device(): cross_total = lax.psum(cross_part, ('row', 'col'))  129 us
    another operation x6, other arithmetic, tri_solve(): return jax.scipy.linalg.solve_triangular(factor, values, lower=True)  79.2 us
    psum x2, waiting for transfers between devices, spread(): return lax.psum(jnp.where(mine, array, jnp.zeros_like(array)), axis)  68.1 us
    psum x2, waiting for transfers between devices, backward(): return lax.psum(partial_value, 'row')  64.2 us
  transfers between devices with their start and end apart: 15, of which 15 were waited for; matrix products, arithmetic and copies ran while one was open for 0% of the time, Pallas kernels for 0%

profile of v1, /device:TPU:0, one launch (start us, length us, event | category | flops | bytes accessed | tf_op | source)
XLA Modules:
  0.0 1466.5 jit_solution(9582352364889395421)
XLA Ops:
  11.2 8.9 all_gather.27
  20.0 3.1 fusion.159
  23.2 65.1 %reduce-scatter.5.cloned.1.call-done = f32[64,512]{1,0:T(8,128)} async-done(((f32[512,512]{1,0:T(8,128)}), f32[64,512]{1,0:T(8,128)}) %reduce-scatter.5.cloned.1.call-update) | async-done | bytes 131088 | tf_op jit(solution)/shard_map/reduce_scatter | solution.py:12
  88.4 41.3 %all-gather.9.cloned.1.call-done = f32[512,512]{1,0:T(8,128)} async-done(((f32[64,512]{1,0:T(8,128)}), f32[512,512]{1,0:T(8,128)}) %all-gather.9.cloned.1.call-update) | async-done | bytes 1048592 | tf_op jit(solution)/shard_map/all_gather | solution.py:50
  129.7 4.1 fusion.157
  134.0 32.0 %all-reduce.8.cloned.1.call-done = f32[256,512]{0,1:T(8,128)} async-done(((f32[256,512]{0,1:T(8,128)}), f32[256,512]{0,1:T(8,128)}) %all-reduce.8.cloned.1.call-update) | async-done | bytes 524304 | tf_op jit(solution)/shard_map/psum | solution.py:66
  166.0 3.3 fusion.22
  169.4 65.5 %reduce-scatter.7.cloned.1.call-done = f32[64,512]{1,0:T(8,128)} async-done(((f32[512,512]{1,0:T(8,128)}), f32[64,512]{1,0:T(8,128)}) %reduce-scatter.7.cloned.1.call-update) | async-done | bytes 131088 | tf_op jit(solution)/shard_map/reduce_scatter | solution.py:12
  234.9 1.6 multiply_subtract_fusion.1
  236.6 40.1 %all-gather.11.cloned.1.call-done = f32[512,512]{1,0:T(8,128)} async-done(((f32[64,512]{1,0:T(8,128)}), f32[512,512]{1,0:T(8,128)}) %all-gather.11.cloned.1.call-update) | async-done | bytes 1048592 | tf_op jit(solution)/shard_map/all_gather | solution.py:50
  276.7 1.9 dynamic-slice_select_fusion.1
  278.6 33.0 %all-reduce.10.cloned.1.call-done = f32[256,512]{1,0:T(8,128)} async-done(((f32[256,512]{1,0:T(8,128)}), f32[256,512]{1,0:T(8,128)}) %all-reduce.10.cloned.1.call-update) | async-done | bytes 524304 | tf_op jit(solution)/shard_map/psum | solution.py:17
  311.6 3.0 fusion.73
  314.7 194.8 %all-gather.17.cloned.1.call-done = f32[16384,512]{1,0:T(8,128)} async-done(((f32[512,512]{1,0:T(8,128)}), f32[16384,512]{1,0:T(8,128)}) %all-gather.17.cloned.1.call-update) | async-done | bytes 33554448 | tf_op jit(solution)/shard_map/all_gather | solution.py:85
  509.5 12.4 reduce_sum.18
  523.0 11.7 cholesky.286
  534.8 9.8 custom-call.36
  545.3 11.7 cholesky.305
  557.1 10.2 custom-call.37
  567.9 11.7 cholesky.326
  580.4 9.8 custom-call.38
  590.8 11.9 cholesky.343
  606.7 8.5 while.9
  607.4 1.4 bitcast_dynamic-update-slice_fusion.4
  609.5 1.4 bitcast_dynamic-update-slice_fusion.4
  611.6 1.4 bitcast_dynamic-update-slice_fusion.4
  613.8 1.4 bitcast_dynamic-update-slice_fusion.4
  615.2 39.3 %custom-call.39 = f32[4,128,128]{1,2,0:T(8,128)S(1)} custom-call(f32[4,128,128]{2,1,0:T(8,128)S(1)} %get-tuple-element.42), custom_call_target="InvertDiagBlocksLowerTriangular" | custom-call | tf_op jit(solution)/shard_map/jit(_solve_triangular)/triangular_solve | solution.py:25
  657.4 1.5 convolution_subtract_fusion.12
  659.2 1.7 convolution_subtract_fusion.11
  661.2 3.1 fusion.35
  664.4 62.4 %reduce-scatter.9.cloned.1.call-done = f32[64,512]{1,0:T(8,128)} async-done(((f32[512,512]{1,0:T(8,128)}), f32[64,512]{1,0:T(8,128)}) %reduce-scatter.9.cloned.1.call-update) | async-done | bytes 131088 | tf_op jit(solution)/shard_map/reduce_scatter | solution.py:12
  726.9 41.3 %all-gather.13.cloned.1.call-done = f32[512,512]{1,0:T(8,128)} async-done(((f32[64,512]{1,0:T(8,128)}), f32[512,512]{1,0:T(8,128)}) %all-gather.13.cloned.1.call-update) | async-done | bytes 1048592 | tf_op jit(solution)/shard_map/all_gather | solution.py:50
  768.2 4.1 fusion.153
  772.4 32.2 %all-reduce.12.cloned.1.call-done = f32[256,512]{0,1:T(8,128)} async-done(((f32[256,512]{0,1:T(8,128)}), f32[256,512]{0,1:T(8,128)}) %all-reduce.12.cloned.1.call-update) | async-done | bytes 524304 | tf_op jit(solution)/shard_map/psum | solution.py:66
  804.6 3.3 fusion.20
  808.0 65.6 %reduce-scatter.11.cloned.1.call-done = f32[64,512]{1,0:T(8,128)} async-done(((f32[512,512]{1,0:T(8,128)}), f32[64,512]{1,0:T(8,128)}) %reduce-scatter.11.cloned.1.call-update) | async-done | bytes 131088 | tf_op jit(solution)/shard_map/reduce_scatter | solution.py:12
  873.6 1.6 multiply_subtract_fusion
  875.3 40.1 %all-gather.15.cloned.1.call-done = f32[512,512]{1,0:T(8,128)} async-done(((f32[64,512]{1,0:T(8,128)}), f32[512,512]{1,0:T(8,128)}) %all-gather.15.cloned.1.call-update) | async-done | bytes 1048592 | tf_op jit(solution)/shard_map/all_gather | solution.py:50
  915.4 3.4 fusion.150
  918.8 1.9 dynamic-slice_select_fusion
  920.7 35.1 %all-reduce.16.cloned.1.call-done = (f32[256,512]{1,0:T(8,128)}, f32[256,512]{1,0:T(8,128)}) async-done(((f32[256,512]{1,0:T(8,128)}, f32[256,512]{1,0:T(8,128)}), (f32[256,512]{1,0:T(8,128)}, f32[256,512]{1,0:T(8,128)})) %all-reduce.16.cloned.1.call-update) | async-done | bytes 1048592 | tf_op jit(solution)/shard_map/psum | solution.py:17
  955.9 3.0 fusion.75
  958.9 3.0 fusion.78
  962.9 129.2 %all-reduce.14.cloned.1.call-done = f32[512,512]{0,1:T(8,128)} async-done(((f32[512,512]{0,1:T(8,128)}), f32[512,512]{0,1:T(8,128)}) %all-reduce.14.cloned.1.call-update) | async-done | bytes 1048592 | tf_op jit(solution)/shard_map/psum | solution.py:87
  1092.1 2.3 broadcast_multiply_fusion
  1094.4 194.2 %all-gather.19.cloned.1.call-done = f32[16384,512]{1,0:T(8,128)} async-done(((f32[512,512]{1,0:T(8,128)}), f32[16384,512]{1,0:T(8,128)}) %all-gather.19.cloned.1.call-update) | async-done | bytes 33554448 | tf_op jit(solution)/shard_map/all_gather | solution.py:85
  1288.6 12.7 reduce_sum.19
  1302.4 11.7 cholesky.358
  1314.2 9.8 custom-call.40
  1324.7 11.7 cholesky.377
  1337.7 9.9 custom-call.41
  1348.4 11.7 cholesky.398
  1360.8 9.8 custom-call.42
  1371.2 11.7 cholesky.415
  1386.3 8.0 while.10
  1394.3 39.5 %custom-call.43 = f32[4,128,128]{1,2,0:T(8,128)S(1)} custom-call(f32[4,128,128]{2,1,0:T(8,128)S(1)} %get-tuple-element.43), custom_call_target="InvertDiagBlocksLowerTriangular" | custom-call | tf_op jit(solution)/shard_map/jit(_solve_triangular)/triangular_solve | solution.py:25
  1436.9 1.5 convolution_subtract_fusion.3
  1438.8 2.0 convolution_subtract_fusion.2
  1441.2 2.4 convolution_subtract_fusion.5
  1447.1 1.5 convolution_subtract_fusion.4
  1451.8 1.5 convolution_subtract_fusion.9
  1453.6 1.7 convolution_subtract_fusion.8
  1457.2 1.8 convolution_subtract_fusion.16
  (136 shorter events, 41.9 us)
Async XLA Ops:
  7.2 81.1 %reduce-scatter.5.cloned.1.call-start = ((), (), s32[]{:S(2)}) async-start(), calls=%async_computation.4 | async-start | bytes 1179648 | tf_op jit(solution)/shard_map/reduce_scatter | solution.py:12
  23.1 106.5 %all-gather.9.cloned.1.call-start = ((), (), s32[]{:S(2)}) async-start(), calls=%async_computation.5 | async-start | bytes 1179648 | tf_op jit(solution)/shard_map/all_gather | solution.py:50
  88.3 77.7 %all-reduce.8.cloned.1.call-start = ((), (), s32[]{:S(2)}) async-start(), calls=%async_computation.6 | async-start | bytes 1048576 | tf_op jit(solution)/shard_map/psum | solution.py:66
  133.8 101.1 %reduce-scatter.7.cloned.1.call-start = ((), (), s32[]{:S(2)}) async-start(), calls=%async_computation.7 | async-start | bytes 1179648 | tf_op jit(solution)/shard_map/reduce_scatter | solution.py:12
  169.3 107.3 %all-gather.11.cloned.1.call-start = ((), (), s32[]{:S(2)}) async-start(), calls=%async_computation.8 | async-start | bytes 1179648 | tf_op jit(solution)/shard_map/all_gather | solution.py:50
  236.6 75.0 %all-reduce.10.cloned.1.call-start = ((), (), s32[]{:S(2)}) async-start(), calls=%async_computation.9 | async-start | bytes 1048576 | tf_op jit(solution)/shard_map/psum | solution.py:17
  278.6 230.9 %all-gather.17.cloned.1.call-start = ((), (), s32[]{:S(2)}) async-start(), calls=%async_computation.16 | async-start | bytes 34603008 | tf_op jit(solution)/shard_map/all_gather | solution.py:85
  314.6 412.2 %reduce-scatter.9.cloned.1.call-start = ((), (), s32[]{:S(2)}) async-start(), calls=%async_computation.10 | async-start | bytes 1179648 | tf_op jit(solution)/shard_map/reduce_scatter | solution.py:12
  664.4 103.9 %all-gather.13.cloned.1.call-start = ((), (), s32[]{:S(2)}) async-start(), calls=%async_computation.11 | async-start | bytes 1179648 | tf_op jit(solution)/shard_map/all_gather | solution.py:50
  726.9 77.7 %all-reduce.12.cloned.1.call-start = ((), (), s32[]{:S(2)}) async-start(), calls=%async_computation.12 | async-start | bytes 1048576 | tf_op jit(solution)/shard_map/psum | solution.py:66
  772.3 101.2 %reduce-scatter.11.cloned.1.call-start = ((), (), s32[]{:S(2)}) async-start(), calls=%async_computation.13 | async-start | bytes 1179648 | tf_op jit(solution)/shard_map/reduce_scatter | solution.py:12
  807.9 107.5 %all-gather.15.cloned.1.call-start = ((), (), s32[]{:S(2)}) async-start(), calls=%async_computation.14 | async-start | bytes 1179648 | tf_op jit(solution)/shard_map/all_gather | solution.py:50
  875.2 80.7 %all-reduce.16.cloned.1.call-start = ((), (), s32[]{:S(2)}) async-start(), calls=%async_computation.18 | async-start | bytes 2097152 | tf_op jit(solution)/shard_map/psum | solution.py:17
  920.7 171.4 %all-reduce.14.cloned.1.call-start = ((), (), s32[]{:S(2)}) async-start(), calls=%async_computation.15 | async-start | bytes 2097152 | tf_op jit(solution)/shard_map/psum | solution.py:87
  958.9 329.8 %all-gather.19.cloned.1.call-start = ((), (), s32[]{:S(2)}) async-start(), calls=%async_computation.17 | async-start | bytes 34603008 | tf_op jit(solution)/shard_map/all_gather | solution.py:85
Sparse Core Ops, SparseCore 0:
  23.3 65.0 reduce-scatter.4
  90.4 39.1 all-gather.8
  133.9 32.0 all-reduce.7
  169.9 64.9 reduce-scatter.6
  237.4 39.1 all-gather.10
  279.4 32.0 all-reduce.9
  315.1 194.2 all-gather.16
  664.5 62.3 reduce-scatter.8
  729.0 39.2 all-gather.12
  772.5 32.0 all-reduce.11
  808.6 64.9 reduce-scatter.10
  876.1 39.2 all-gather.14
  920.8 35.0 all-reduce.15
  960.9 131.1 all-reduce.13
  1095.5 193.1 all-gather.18
